TPU v7x, 32 devices: a whole 2x2x4 slice. The times are simulated.
32 devices in a mesh: dp: 1, vocab: 32 (over z, y, x, core).
Axes of the slice: x: 2, y: 2, z: 4, core: 2. Of those that a mesh axis runs over, the one named last changes fastest.
Arguments:
- input_ids: int32 [256], P('dp'), may hold values from 0 to 63999
- target_ids: int32 [256], P('dp'), may hold values from 0 to 63999
- loss_mask: int32 [256], P('dp'), may hold values 0 or 1
- final_hidden: bfloat16 [256, 3584], P('dp'), may hold values from -5 to 5, as said below
- norm_gain: float32 [3584], replicated, may hold values from 0.25 to 1.75
- embed_cotangent: bfloat16 [256, 3584], P('dp'), may hold values from -0.059814453 to 0.059814453
- table: bfloat16 [64000, 3584], P(('dp', 'vocab')), may hold values from -0.08351914 to 0.08351914, as said below
Outputs:
- embedded: bfloat16 [256, 3584], P('dp')
- loss: float32 [], replicated
- grad_hidden: bfloat16 [256, 3584], P('dp')
- gain_grad: float32 [3584], replicated
- table_grad: bfloat16 [64000, 3584], P(('dp', 'vocab'))
Inputs may be any that keep to these rules, and one draw needn't show every extreme that they name: Every entry of table lies within -5 / sqrt(3584) and 5 / sqrt(3584). Every entry of final_hidden lies within -5 and 5.
All inputs are finite; a program needn't handle non-finite values.
Results may differ from a plain program's by a relative error of at most 0.003.
Values may be sent and summed in bfloat16 or wider, within the bound.
A program may use at most 256 MiB of HBM per device.

v0:
```python
import math
import jax
import jax.numpy as jnp
from jax import lax
from jax.sharding import PartitionSpec as P

SOFTCAP = 30
EPSILON = 1e-06


def norm_backward(upstream, widened, inv_rms, norm_gain):
    scaled_up = upstream * norm_gain
    mean_dot = jnp.mean(scaled_up * widened, axis=1, keepdims=True)
    gradient = inv_rms * scaled_up - widened * (inv_rms * inv_rms * inv_rms) * mean_dot
    gain_part = jnp.sum(upstream * widened * inv_rms, axis=0)
    return (gradient.astype(jnp.bfloat16), gain_part)


def body(input_ids, target_ids, loss_mask, final_hidden, norm_gain, embed_cotangent, table):
    row_count = table.shape[0]
    embed_scale = math.sqrt(table.shape[1])
    owner = lax.axis_index(("dp", "vocab"))
    first_row = owner * row_count
    every_id, every_target, every_mask = (
        lax.all_gather(input_ids, "dp", axis=0, tiled=True),
        lax.all_gather(target_ids, "dp", axis=0, tiled=True),
        lax.all_gather(loss_mask, "dp", axis=0, tiled=True),
    )
    token_total = every_id.shape[0]
    per_group = token_total // lax.axis_size("dp")
    share_rows = token_total // lax.axis_size(("dp", "vocab"))
    widened = final_hidden.astype(jnp.float32)
    inv_rms = lax.rsqrt(jnp.mean(widened * widened, axis=1, keepdims=True) + EPSILON)
    normed = (widened * inv_rms * norm_gain).astype(jnp.bfloat16)
    normed_all, cotangent_all = (
        lax.all_gather(normed, "dp", axis=0, tiled=True),
        lax.all_gather(embed_cotangent, "dp", axis=0, tiled=True),
    )

    def lookup_term():
        wanted = lax.slice_in_dim(every_id, 0, per_group * lax.axis_size("dp"), axis=0) - first_row
        inside = (wanted >= 0) & (wanted < row_count)
        picked = jnp.take(table, jnp.clip(wanted, 0, row_count - 1), axis=0)
        return jnp.where(inside[:, None], picked.astype(jnp.float32), 0.0)

    group_rows = lax.psum_scatter(
        lookup_term().astype(jnp.bfloat16), "dp", scatter_dimension=0, tiled=True
    ).astype(jnp.float32)
    found = lax.psum(group_rows.astype(jnp.bfloat16), "vocab").astype(jnp.float32)
    embedded = (found * embed_scale).astype(jnp.bfloat16)
    raw_logits = lax.dot_general(
        normed_all, table, (((1,), (1,)), ((), ())), preferred_element_type=jnp.float32
    )
    capped = SOFTCAP * jnp.tanh(raw_logits / SOFTCAP)
    exp_logits = jnp.exp(capped)
    local_targets = every_target - first_row
    target_hit = lax.broadcasted_iota(jnp.int32, capped.shape, 1) == local_targets[:, None]
    token_weight = every_mask.astype(jnp.float32)
    picked_sum = jnp.sum(token_weight * jnp.sum(jnp.where(target_hit, capped, 0.0), axis=1))
    sum_exp, target_sum = lax.psum((jnp.sum(exp_logits, axis=1), picked_sum), ("dp", "vocab"))
    loss = (jnp.sum(token_weight * jnp.log(sum_exp)) - target_sum) / jnp.maximum(
        jnp.sum(token_weight), 1.0
    )
    slope = (
        token_weight[:, None]
        * (exp_logits / sum_exp[:, None] - target_hit.astype(jnp.float32))
        * (1.0 - (capped / SOFTCAP) ** 2)
    )
    slope_low = slope.astype(jnp.bfloat16)
    head_part = lax.dot_general(
        slope_low, normed_all, (((0,), (0,)), ((), ())), preferred_element_type=jnp.float32
    )
    local_ids = every_id - first_row
    owned = (local_ids >= 0) & (local_ids < row_count)
    segment_ids = jnp.where(owned, local_ids, row_count)
    embed_part = (
        jax.ops.segment_sum(
            cotangent_all.astype(jnp.float32), segment_ids, num_segments=row_count + 1
        )[:row_count]
        * embed_scale
    )
    table_grad = (head_part + embed_part).astype(jnp.bfloat16)

    def upstream_term():
        block = lax.slice_in_dim(slope_low, 0, share_rows * lax.axis_size(("dp", "vocab")), axis=0)
        return jnp.dot(block, table, preferred_element_type=jnp.float32)

    upstream = lax.psum_scatter(upstream_term(), ("dp", "vocab"), scatter_dimension=0, tiled=True)
    offset_rows = lax.axis_index("vocab") * share_rows
    widened_share = lax.dynamic_slice_in_dim(widened, offset_rows, share_rows, 0)
    inv_share = lax.dynamic_slice_in_dim(inv_rms, offset_rows, share_rows, 0)
    gradient_share, gain_part = norm_backward(upstream, widened_share, inv_share, norm_gain)
    gain_grad = lax.psum(gain_part, ("dp", "vocab"))
    grad_hidden = lax.all_gather(gradient_share, "vocab", axis=0, tiled=True)
    return (embedded, loss, grad_hidden, gain_grad, table_grad)


def solution(mesh):
    placed = (
        P("dp"),
        P("dp"),
        P("dp"),
        P("dp", None),
        P(),
        P("dp", None),
        P(("dp", "vocab"), None),
    )
    return jax.shard_map(
        body,
        mesh=mesh,
        in_specs=placed,
        out_specs=(P("dp", None), P(), P("dp", None), P(), P(("dp", "vocab"), None)),
        check_vma=False,
    )
```

profile of v0, /device:TPU:0, one launch (start us, length us, event | category | flops | bytes accessed | tf_op | source)
XLA Modules:
  0.0 414.2 jit_solution(4255250760945379497)
XLA Ops:
  7.2 0.0 reduce-scatter.2.cloned.1.call-start
  7.2 1.9 multiply_reduce_fusion
  9.2 0.7 broadcast_subtract_fusion
  9.9 0.0 copy-start.4
  9.9 8.1 %select_reduce_fusion = (f32[256]{0:T(256)S(1)}, f32[256]{0:T(256)S(1)}, f32[256,2000]{0,1:T(8,128)S(1)}) fusion(s32[256]{0:T(256)S(1)} %broadcast_subtract_fusion, bf16[2000,3584]{1,0:T(8,128)(2,1)} %param.13, f32[3584]{0:T(1024)} %param.11, f32[256]{0:T(256)S(1)} %add_rsqrt_fusion, bf16[256,3584]{1,0:T(8,128)(2,1)} %param.10), kind=kOutput, calls=%fused_computation.15 | convolution fusion | flops 3676757504 | bytes 18237440 | tf_op jit(solution)/shard_map/dot_general | solution.py:51
  18.0 0.0 copy-start.1
  18.0 42.0 %psum.29 = f32[256]{0:T(256)S(1)} all-reduce(f32[256]{0:T(256)S(1)} %get-tuple-element.8), channel_id=1, replica_groups=mesh['dp'=1,'vocab'=32] {'dp','vocab'}, use_global_device_ids=true, to_apply=%region_3.4 | all-reduce | flops 256 | bytes 2048 | tf_op jit(solution)/shard_map/psum | solution.py:60
  60.0 0.0 copy-done.4
  60.0 9.4 %fusion.7 = f32[256,3584]{1,0:T(8,128)} fusion(bf16[2000,3584]{1,0:T(8,128)(2,1)} %param.13, f32[256,2000]{0,1:T(8,128)S(1)} %get-tuple-element.19, f32[256]{0:T(256)S(1)} %psum.29, f32[256]{0:T(256)S(1)} %convert_element_type.42, s32[256]{0:T(256)S(1)} %broadcast_subtract_fusion), kind=kOutput, calls=%fused_computation.34 | convolution fusion | flops 3675136000 | bytes 20057088 | tf_op jit(solution)/shard_map/dot_general | solution.py:86
  69.3 0.0 copy-done.1
  69.3 0.0 copy-start.3
  69.3 0.0 reduce-scatter.2.cloned.1.call-update
  69.4 0.0 all-reduce.3.cloned.1.call-start
  69.4 0.6 copy-done.3
  70.0 11.7 %gather_fusion = bf16[256,3584]{1,0:T(8,128)(2,1)} fusion(bf16[2000,3584]{1,0:T(8,128)(2,1)} %param.13, s32[1024]{0:T(1024)S(1)} %pad_clamp_fusion), kind=kCustom, calls=%fused_computation | custom fusion | bytes 3671040 | tf_op jit(solution)/shard_map/jit(_take)/gather | solution.py:43
  81.7 0.0 copy-start
  81.7 3.9 select_convert_fusion
  85.6 0.0 all-reduce.3.cloned.1.call-update
  85.6 0.0 copy-start.2
  85.6 0.2 all-gather.2.cloned.1.call-start
  85.9 0.0 copy-done
  85.9 2.2 convert_element_type.43
  88.1 0.1 fusion.6
  88.2 0.6 convert_reduce_fusion
  89.5 121.3 %reduce-scatter.2.cloned.1.call-done = f32[8,3584]{1,0:T(8,128)} async-done(((f32[256,3584]{1,0:T(8,128)}), f32[8,3584]{1,0:T(8,128)}) %reduce-scatter.2.cloned.1.call-update) | async-done | bytes 114704 | tf_op jit(solution)/shard_map/reduce_scatter | solution.py:88
  210.7 0.0 copy-done.2
  210.7 1.2 multiply_reduce_fusion.1
  211.9 1.7 subtract_convert_fusion
  213.6 0.0 all-gather.2.cloned.1.call-update
  213.6 18.1 %scatter_custom_fusion = f32[2001,3584]{1,0:T(8,128)} fusion(s32[256]{0:T(256)S(1)} %subtract_select_fusion, f32[]{:T(128)} %constant.21.clone.1, bf16[256,3584]{1,0:T(8,128)(2,1)} %param.12), kind=kCustom, calls=%fused_computation.5 | custom fusion | flops 1835008 | bytes 30521348 | tf_op jit(solution)/shard_map/scatter-add | solution.py:77
  231.7 17.1 %fusion.1 = bf16[2000,3584]{1,0:T(8,128)(2,1)} fusion(f32[2001,3584]{1,0:T(8,128)} %scatter_custom_fusion, f32[3584]{0:T(1024)S(1)} %copy-done.2, f32[256]{0:T(256)S(1)} %add_rsqrt_fusion, bf16[256,3584]{1,0:T(8,128)(2,1)S(1)} %copy-done, f32[256,2000]{0,1:T(8,128)} %copy-done.1, f32[256]{0:T(256)S(1)} %psum.29, f32[256]{0:T(256)S(1)} %convert_element_type.42, ...), kind=kOutput, calls=%fused_computation.4 | convolution fusion | flops 3700310016 | bytes 46909440 | tf_op jit(solution)/shard_map/dot_general | solution.py:70
  248.8 97.3 %all-reduce.3.cloned.1.call-done = bf16[256,3584]{1,0:T(8,128)(2,1)} async-done(((bf16[256,3584]{1,0:T(8,128)(2,1)}), bf16[256,3584]{1,0:T(8,128)(2,1)}) %all-reduce.3.cloned.1.call-update) | async-done | bytes 1835024 | tf_op jit(solution)/shard_map/psum | solution.py:49
  346.2 3.0 multiply_convert_fusion.1
  349.2 39.6 %all-reduce = (f32[]{:T(128)}, f32[3584]{0:T(1024)}) all-reduce(f32[]{:T(128)} %get-tuple-element.11, f32[3584]{0:T(1024)S(1)} %get-tuple-element.5), channel_id=1, replica_groups=mesh['dp'=1,'vocab'=32] {'dp','vocab'}, use_global_device_ids=true, to_apply=%region_7.8 | all-reduce | flops 3585 | bytes 28680 | tf_op jit(solution)/shard_map/psum | solution.py:60
  390.1 13.7 %all-gather.2.cloned.1.call-done = bf16[256,3584]{1,0:T(8,128)(2,1)} async-done(((bf16[8,3584]{1,0:T(8,128)(2,1)}), bf16[256,3584]{1,0:T(8,128)(2,1)}) %all-gather.2.cloned.1.call-update) | async-done | bytes 1835024 | tf_op jit(solution)/shard_map/all_gather | solution.py:94
  403.7 2.8 copy.14
  (6 shorter events, 0.0 us)
Async XLA Ops:
  7.2 203.6 %reduce-scatter.2.cloned.1.call-start = ((), (), s32[]{:S(2)}) async-start(), calls=%async_computation.2 | async-start | bytes 3784704 | tf_op jit(solution)/shard_map/reduce_scatter | solution.py:88
  9.9 50.1 %copy-start.4 = (s32[256]{0:T(256)S(1)}, s32[256]{0:T(256)}, u32[]{:S(2)}) copy-start(s32[256]{0:T(256)} %param.9) | copy-start | bytes 3076
  18.0 51.4 %copy-start.1 = (f32[256,2000]{0,1:T(8,128)}, f32[256,2000]{0,1:T(8,128)S(1)}, u32[]{:S(2)}) copy-start(f32[256,2000]{0,1:T(8,128)S(1)} %get-tuple-element.19) | copy-start | bytes 6144004
  69.3 0.7 copy-start.3
  69.4 276.8 %all-reduce.3.cloned.1.call-start = ((), (), s32[]{:S(2)}) async-start(), calls=%async_computation.1 | async-start | bytes 3670016 | tf_op jit(solution)/shard_map/psum | solution.py:49
  81.7 4.1 copy-start
  85.6 125.1 %copy-start.2 = (f32[3584]{0:T(1024)S(1)}, f32[3584]{0:T(1024)}, u32[]{:S(2)}) copy-start(f32[3584]{0:T(1024)} %param.11) | copy-start | bytes 43012
  85.6 318.1 %all-gather.2.cloned.1.call-start = ((), (), s32[]{:S(2)}) async-start(), calls=%async_computation.3 | async-start | bytes 1892352 | tf_op jit(solution)/shard_map/all_gather | solution.py:94
Sparse Core Ops, SparseCore 0:
  69.5 141.1 reduce-scatter.1
  216.6 129.4 all-reduce.2
  349.0 54.6 all-gather.1
where the time goes:
time: 415 us; the launch traced here: 414 us
  waiting for transfers between devices  232 us (56%)
  blocking collectives  81.6 us (20%)
  matrix products  34.6 us (8%)
  other arithmetic  33.4 us (8%)
  between operations  16.9 us (4%)
  local copies, waits for them, and re-layouts  15.1 us (4%)
    reduce_scatter x1, waiting for transfers between devices, body(): lax.psum_scatter(upstream_term(), ('dp', 'vocab'), scatter_dimension=0, t...  121 us
    psum x1, waiting for transfers between devices, body(): lax.psum(group_rows.astype(jnp.bfloat16), 'vocab').astype(jnp.float32)  97.3 us
    psum x2, blocking collectives, body(): lax.psum((jnp.sum(exp_logits, axis=1), picked_sum), ('dp', 'vocab'))  81.6 us
    scatter-add x1, other arithmetic, body(): jax.ops.segment_sum(cotangent_all.astype(jnp.float32), segment_ids, num_s...  18.1 us
    dot_general x1, matrix products, body(): lax.dot_general(slope_low, normed_all, (((0,), (0,)), ((), ())), preferre...  17.1 us
    all_gather x1, waiting for transfers between devices, body(): grad_hidden = lax.all_gather(gradient_share, 'vocab', axis=0, tiled=True)  13.7 us
    gather x1, local copies, waits for them, and re-layouts, lookup_term(): picked = jnp.take(table, jnp.clip(wanted, 0, row_count - 1), axis=0)  11.7 us
    dot_general x1, matrix products, upstream_term(): return jnp.dot(block, table, preferred_element_type=jnp.float32)  9.38 us
  transfers between devices with their start and end apart: 3, of which 3 were waited for; matrix products, arithmetic and copies ran while one was open for 14% of the time, Pallas kernels for 0%

commit v1 on v0

--- a/solution.py
+++ b/solution.py
@@ -6,6 +6,11 @@
 
 SOFTCAP = 30
 EPSILON = 1e-06
+
+
+def add_all(x, name):
+    terms = lax.all_gather(x, name)
+    return jnp.sum(terms, axis=0)
 
 
 def norm_backward(upstream, widened, inv_rms, norm_gain):
@@ -46,7 +51,7 @@
     group_rows = lax.psum_scatter(
         lookup_term().astype(jnp.bfloat16), "dp", scatter_dimension=0, tiled=True
     ).astype(jnp.float32)
-    found = lax.psum(group_rows.astype(jnp.bfloat16), "vocab").astype(jnp.float32)
+    found = add_all(group_rows.astype(jnp.bfloat16), "vocab").astype(jnp.float32)
     embedded = (found * embed_scale).astype(jnp.bfloat16)
     raw_logits = lax.dot_general(
         normed_all, table, (((1,), (1,)), ((), ())), preferred_element_type=jnp.float32

time: 415 us -> 620 us (1.49)
  waiting for transfers between devices: 232 us -> 413 us
  other arithmetic: 33.4 us -> 51 us
    all_gather x0 -> x1, waiting for transfers between devices: none -> 276 us  [add_all(): terms = lax.all_gather(x, name)]
    psum x1 -> x0, waiting for transfers between devices: 97.3 us -> none  [body(): lax.psum(group_rows.astype(jnp.bfloat16), 'vocab').astype(jnp.float32)]
    reduce_sum x0 -> x1, other arithmetic: none -> 19.2 us  [add_all(): return jnp.sum(terms, axis=0)]
    reduce_scatter x1, waiting for transfers between devices: 121 us -> 137 us  [body(): lax.psum_scatter(upstream_term(), ('dp', 'vocab'), scatter_dimension=0, t...]
    all_gather x1, waiting for transfers between devices: 13.7 us -> 0.02 us  [body(): grad_hidden = lax.all_gather(gradient_share, 'vocab', axis=0, tiled=True)]
  transfers between devices with their start and end apart: 3 -> 3, of which waited for: 3 -> 2; matrix products, arithmetic and copies ran while one was open for 14% -> 9% of each run, Pallas kernels for 0% -> 0%
where the time goes in v1:
time: 620 us
  waiting for transfers between devices  413 us (67%)
  blocking collectives  82.8 us (13%)
  other arithmetic  51 us (8%)
  matrix products  40.6 us (7%)
  between operations  16.9 us (3%)
  local copies, waits for them, and re-layouts  14.9 us (2%)
    all_gather x1, waiting for transfers between devices, add_all(): terms = lax.all_gather(x, name)  276 us
    reduce_scatter x1, waiting for transfers between devices, body(): lax.psum_scatter(upstream_term(), ('dp', 'vocab'), scatter_dimension=0, t...  137 us
    psum x2, blocking collectives, body(): lax.psum((jnp.sum(exp_logits, axis=1), picked_sum), ('dp', 'vocab'))  82.8 us
    reduce_sum x1, other arithmetic, add_all(): return jnp.sum(terms, axis=0)  19.2 us
    scatter-add x1, other arithmetic, body(): jax.ops.segment_sum(cotangent_all.astype(jnp.float32), segment_ids, num_s...  18 us
    dot_general x1, matrix products, body(): lax.dot_general(slope_low, normed_all, (((0,), (0,)), ((), ())), preferre...  17.3 us
  transfers between devices with their start and end apart: 3, of which 2 were waited for; matrix products, arithmetic and copies ran while one was open for 9% of the time, Pallas kernels for 0%

profile of v1, /device:TPU:0, one launch (start us, length us, event | category | flops | bytes accessed | tf_op | source)
XLA Modules:
  0.0 619.9 jit_solution(6515225682340192654)
XLA Ops:
  7.2 0.0 reduce-scatter.2.cloned.1.call-start
  7.2 1.9 multiply_reduce_fusion
  9.2 0.7 broadcast_subtract_fusion
  9.9 0.0 copy-start.4
  9.9 11.6 %select_reduce_fusion = (f32[256]{0:T(256)S(1)}, f32[256]{0:T(256)S(1)}, f32[256,2000]{0,1:T(8,128)}) fusion(s32[256]{0:T(256)S(1)} %broadcast_subtract_fusion, bf16[2000,3584]{1,0:T(8,128)(2,1)} %param.13, f32[3584]{0:T(1024)} %param.11, f32[256]{0:T(256)S(1)} %add_rsqrt_fusion, bf16[256,3584]{1,0:T(8,128)(2,1)} %param.10), kind=kOutput, calls=%fused_computation.15 | convolution fusion | flops 3676757504 | bytes 18237440 | tf_op jit(solution)/shard_map/dot_general | solution.py:56
  21.4 41.9 %psum.21 = f32[256]{0:T(256)S(1)} all-reduce(f32[256]{0:T(256)S(1)} %get-tuple-element.8), channel_id=1, replica_groups=mesh['dp'=1,'vocab'=32] {'dp','vocab'}, use_global_device_ids=true, to_apply=%region_3.4 | all-reduce | flops 256 | bytes 2048 | tf_op jit(solution)/shard_map/psum | solution.py:65
  63.3 0.0 copy-done.4
  63.3 11.7 %fusion.7 = f32[256,3584]{1,0:T(8,128)} fusion(bf16[2000,3584]{1,0:T(8,128)(2,1)} %param.13, f32[256,2000]{0,1:T(8,128)} %get-tuple-element.19, f32[256]{0:T(256)S(1)} %psum.21, f32[256]{0:T(256)S(1)} %convert_element_type.58, s32[256]{0:T(256)S(1)} %broadcast_subtract_fusion), kind=kOutput, calls=%fused_computation.35 | convolution fusion | flops 3675136000 | bytes 20057088 | tf_op jit(solution)/shard_map/dot_general | solution.py:91
  75.1 0.0 copy-start
  75.1 0.0 reduce-scatter.2.cloned.1.call-update
  75.1 0.0 copy-start.2
  75.1 0.0 copy-start.3
  75.1 0.0 all-gather.5.cloned.1.call-start
  75.2 1.4 copy-done
  76.6 2.2 convert_element_type.59
  78.8 0.1 fusion.6
  78.9 137.4 %reduce-scatter.2.cloned.1.call-done = f32[8,3584]{1,0:T(8,128)} async-done(((f32[256,3584]{1,0:T(8,128)}), f32[8,3584]{1,0:T(8,128)}) %reduce-scatter.2.cloned.1.call-update) | async-done | bytes 114704 | tf_op jit(solution)/shard_map/reduce_scatter | solution.py:93
  216.3 0.0 copy-done.2
  216.3 1.2 multiply_reduce_fusion.1
  217.4 1.7 subtract_convert_fusion
  219.1 0.0 all-gather.5.cloned.1.call-update
  219.1 0.2 all-gather.3.cloned.1.call-start
  219.4 0.0 copy-done.3
  219.4 11.7 %gather_fusion = bf16[256,3584]{1,0:T(8,128)(2,1)} fusion(bf16[2000,3584]{1,0:T(8,128)(2,1)} %param.13, s32[1024]{0:T(1024)S(1)} %pad_clamp_fusion), kind=kCustom, calls=%fused_computation | custom fusion | bytes 3671040 | tf_op jit(solution)/shard_map/jit(_take)/gather | solution.py:48
  231.1 3.7 select_convert_fusion
  234.8 0.0 all-gather.3.cloned.1.call-update
  234.9 0.7 convert_reduce_fusion
  236.2 18.0 %scatter_custom_fusion = f32[2001,3584]{1,0:T(8,128)} fusion(s32[256]{0:T(256)S(1)} %subtract_select_fusion, f32[]{:T(128)} %constant.22.clone.1, bf16[256,3584]{1,0:T(8,128)(2,1)} %param.12), kind=kCustom, calls=%fused_computation.5 | custom fusion | flops 1835008 | bytes 30521348 | tf_op jit(solution)/shard_map/scatter-add | solution.py:82
  254.3 17.3 %fusion.1 = bf16[2000,3584]{1,0:T(8,128)(2,1)} fusion(f32[2001,3584]{1,0:T(8,128)} %scatter_custom_fusion, f32[3584]{0:T(1024)S(1)} %copy-done.2, f32[256]{0:T(256)S(1)} %add_rsqrt_fusion, bf16[256,3584]{1,0:T(8,128)(2,1)S(1)} %copy-done, f32[256,2000]{0,1:T(8,128)} %get-tuple-element.19, f32[256]{0:T(256)S(1)} %psum.21, f32[256]{0:T(256)S(1)} %convert_element_type.58, ...), kind=kOutput, calls=%fused_computation.4 | convolution fusion | flops 3700310016 | bytes 46909440 | tf_op jit(solution)/shard_map/dot_general | solution.py:75
  271.6 40.9 %all-reduce = (f32[]{:T(128)}, f32[3584]{0:T(1024)}) all-reduce(f32[]{:T(128)} %get-tuple-element.11, f32[3584]{0:T(1024)S(1)} %get-tuple-element.5), channel_id=1, replica_groups=mesh['dp'=1,'vocab'=32] {'dp','vocab'}, use_global_device_ids=true, to_apply=%region_7.8 | all-reduce | flops 3585 | bytes 28680 | tf_op jit(solution)/shard_map/psum | solution.py:65
  313.8 0.0 all-gather.5.cloned.1.call-done
  313.8 275.9 %all-gather.3.cloned.1.call-done = bf16[32,256,3584]{2,1,0:T(8,128)(2,1)} async-done(((bf16[1,256,3584]{2,1,0:T(8,128)(2,1)}), bf16[32,256,3584]{2,1,0:T(8,128)(2,1)}) %all-gather.3.cloned.1.call-update) | async-done | bytes 58720272 | tf_op jit(solution)/shard_map/all_gather | solution.py:12
  589.7 19.2 %reduce_sum.84 = bf16[256,3584]{1,0:T(8,128)(2,1)S(1)} reduce(bf16[32,256,3584]{2,1,0:T(8,128)(2,1)} %all-gather.3.cloned.1.call-done, bf16[]{:T(256)} %constant.23.clone.1), dimensions={0}, to_apply=%region_0.0 | reduce | flops 28442624 | bytes 60555264 | tf_op jit(solution)/shard_map/reduce_sum | solution.py:13
  608.9 0.0 copy-start.1
  608.9 1.5 multiply_convert_fusion.1
  610.5 0.5 copy-done.1
  611.0 1.2 copy.13
  (6 shorter events, 0.0 us)
Async XLA Ops:
  7.2 209.1 %reduce-scatter.2.cloned.1.call-start = ((), (), s32[]{:S(2)}) async-start(), calls=%async_computation.2 | async-start | bytes 3784704 | tf_op jit(solution)/shard_map/reduce_scatter | solution.py:93
  9.9 53.5 %copy-start.4 = (s32[256]{0:T(256)S(1)}, s32[256]{0:T(256)}, u32[]{:S(2)}) copy-start(s32[256]{0:T(256)} %param.9) | copy-start | bytes 3076
  75.1 1.5 copy-start
  75.1 141.2 %copy-start.2 = (f32[3584]{0:T(1024)S(1)}, f32[3584]{0:T(1024)}, u32[]{:S(2)}) copy-start(f32[3584]{0:T(1024)} %param.11) | copy-start | bytes 43012
  75.1 144.3 %copy-start.3 = (s32[256]{0:T(256)S(1)}, s32[256]{0:T(256)}, u32[]{:S(2)}) copy-start(s32[256]{0:T(256)} %param.7) | copy-start | bytes 3076
  75.1 238.7 %all-gather.5.cloned.1.call-start = ((), (), s32[]{:S(2)}) async-start(), calls=%async_computation.3 | async-start | bytes 1892352 | tf_op jit(solution)/shard_map/all_gather | solution.py:99
  219.1 370.6 %all-gather.3.cloned.1.call-start = ((), (), s32[]{:S(2)}) async-start(), calls=%async_computation.1 | async-start | bytes 60555264 | tf_op jit(solution)/shard_map/all_gather | solution.py:12
  608.9 2.1 copy-start.1
Sparse Core Ops, SparseCore 0:
  75.2 140.9 reduce-scatter.1
  219.7 51.5 all-gather.4
  274.7 314.9 all-gather.2
